TPU v7x, 256 devices: a 4x2x16 block of a 4x16x16 slice. The times are simulated.
256 devices in a mesh: groups: 2 (over y), ep: 16 (over z), tp: 4 (over x), dp: 2 (over core).
Axes of the slice: x: 4, y: 2, z: 16, core: 2. Of those that a mesh axis runs over, the one named last changes fastest.
The devices are a block of a 4x16x16 slice.
Arguments:
- hidden: bfloat16 [2048, 7168], P(('groups', 'ep', 'tp', 'dp')), parts along dimension 0, may hold values from -6 to 6
- norm_gain: bfloat16 [7168], replicated, may hold values from 0.099609375 to 1.8984375
- router: bfloat16 [7168, 32], replicated, may hold values from -0.0625 to 0.0625
- expert_ids: int32 [2048, 8], P(('groups', 'ep', 'tp', 'dp')), parts along dimension 0, may hold values from 0 to 31, all different within a row; in each aligned block of 4 rows (0 to 3, 4 to 7, ...) at most 2 rows name the same one
- gate_proj: bfloat16 [32, 7168, 1024], P(('ep', 'dp'), None, 'tp'), may hold values from -0.0625 to 0.0625
- up_proj: bfloat16 [32, 7168, 1024], P(('ep', 'dp'), None, 'tp'), may hold values from -0.0625 to 0.0625
- down_proj: bfloat16 [32, 1024, 7168], P(('ep', 'dp'), 'tp'), may hold values from -0.1875 to 0.1875
Outputs:
- mixed: bfloat16 [2048, 7168], P(('groups', 'ep', 'tp', 'dp')), parts along dimension 0
There are 2 independent parts, one for each index of `groups`. A program takes and returns all parts, laid end to end along the dimension named above; an argument that names none is the same for every part. Nothing has to cross between parts.
Inputs may be any that keep to these rules, and one draw needn't show every extreme that they name: `expert_ids`: each row names 8 different experts. In each aligned block of 4 rows (one micro-batch of one device) no expert is named by more than 2 rows, a bound that some block reaches.
All inputs are finite; a program needn't handle non-finite values.
Results may differ from a plain program's by a relative error of at most 0.008.
Values may be sent and summed in bfloat16 or wider, within the bound.
No kernel may reach another device: no remote copies, remote signals or barrier semaphores. Data moves between devices by JAX's collectives and lax.ppermute only.
A program may use at most 128 MiB of HBM per device.

v0:
```python
import jax
import jax.numpy as jnp
from jax import lax
from jax.sharding import PartitionSpec as P

TOP = 8
MICRO = 2
MB_ROWS = 4


route_scale = 2.827
norm_eps = 1e-06


def normalize(hidden, norm_gain):
    values = hidden.astype(jnp.float32)
    spread = jnp.mean(values * values, axis=-1, keepdims=True)
    return (values * lax.rsqrt(spread + norm_eps) * norm_gain.astype(jnp.float32)).astype(
        jnp.bfloat16
    )


def pick_weights(normed, router, expert_ids):
    logits = jnp.dot(normed, router, preferred_element_type=jnp.float32)
    scores = jax.nn.sigmoid(logits)
    expert_range = jnp.arange(router.shape[1], dtype=jnp.int32)
    onehot = expert_ids[:, :, None] == expert_range[None, None, :]
    chosen = jnp.sum(jnp.where(onehot, scores[:, None, :], 0.0), axis=-1)
    return route_scale * chosen / jnp.sum(chosen, axis=-1, keepdims=True)


def slot_table(block_ids, experts, capacity):
    flat_ids = block_ids.reshape(-1)
    onehot = (flat_ids[:, None] == jnp.arange(experts, dtype=jnp.int32)[None, :]).astype(jnp.int32)
    earlier = jnp.cumsum(onehot, axis=0) - onehot
    slot_rank = jnp.sum(earlier * onehot, axis=1)
    position = flat_ids * capacity + slot_rank
    return position.reshape(block_ids.shape)


def body(hidden, norm_gain, router, expert_ids, gate_proj, up_proj, down_proj):
    ep_count = lax.axis_size("ep")
    dp_count = lax.axis_size("dp")
    experts = ep_count * dp_count
    capacity = min(MB_ROWS, max(2, 2 * MB_ROWS * TOP // experts))
    slot_count = experts * capacity
    feature_count = hidden.shape[1]
    normed = normalize(hidden, norm_gain)
    weights = pick_weights(normed, router, expert_ids)
    outputs = []
    for micro_index in range(MICRO):
        lower = micro_index * MB_ROWS
        block_normed = normed[lower : lower + MB_ROWS]
        block_ids = expert_ids[lower : lower + MB_ROWS]
        block_weights = weights[lower : lower + MB_ROWS]
        position = slot_table(block_ids, experts, capacity)
        slot_hits = position[:, :, None] == jnp.arange(slot_count, dtype=jnp.int32)[None, None, :]
        place_map = jnp.sum(slot_hits.astype(jnp.float32), axis=1).astype(jnp.bfloat16)
        outgoing = lax.dot_general(
            place_map, block_normed, (((0,), (0,)), ((), ())), preferred_element_type=jnp.float32
        ).astype(jnp.bfloat16)
        arrived = lax.all_to_all(
            outgoing.reshape(ep_count * dp_count, capacity, feature_count),
            ("ep", "dp"),
            split_axis=0,
            concat_axis=0,
            tiled=True,
        )
        portion = lax.all_gather(
            arrived.reshape(ep_count, 1, dp_count, capacity, feature_count),
            "tp",
            axis=1,
            tiled=True,
        )
        row_block = portion.reshape(-1, feature_count)
        gate_sum = jnp.dot(row_block, gate_proj[0], preferred_element_type=jnp.float32)
        up_sum = jnp.dot(row_block, up_proj[0], preferred_element_type=jnp.float32)
        active = (jax.nn.silu(gate_sum) * up_sum).astype(jnp.bfloat16)
        partial_rows = jnp.dot(active, down_proj[0], preferred_element_type=jnp.float32)
        partial_value = partial_rows.reshape(portion.shape[:-1] + (feature_count,))
        quarter_total = lax.psum_scatter(
            partial_value.astype(jnp.bfloat16), "tp", scatter_dimension=1, tiled=True
        )
        summed_local = quarter_total.reshape(ep_count * dp_count * capacity, feature_count)
        summed = lax.all_to_all(summed_local, ("ep", "dp"), split_axis=0, concat_axis=0, tiled=True)
        mix_map = jnp.sum(jnp.where(slot_hits, block_weights[:, :, None], 0.0), axis=1)
        expert_sum = jnp.dot(mix_map, summed.astype(jnp.float32), precision=lax.Precision.HIGHEST)
        block_hidden = hidden[lower : lower + MB_ROWS].astype(jnp.float32)
        outputs.append((block_hidden + expert_sum).astype(jnp.bfloat16))
    return jnp.concatenate(outputs, axis=0)


def solution(mesh):
    return jax.shard_map(
        body,
        mesh=mesh,
        in_specs=(
            P(("groups", "ep", "tp", "dp"), None),
            P(),
            P(),
            P(("groups", "ep", "tp", "dp"), None),
            P(("ep", "dp"), None, "tp"),
            P(("ep", "dp"), None, "tp"),
            P(("ep", "dp"), "tp", None),
        ),
        out_specs=P(("groups", "ep", "tp", "dp"), None),
        check_vma=False,
    )
```

profile of v0, /device:TPU:33, one launch (start us, length us, event | category | flops | bytes accessed | tf_op | source)
XLA Modules:
  0.0 367.2 jit_solution(15070046716270853434)
XLA Ops:
  6.6 0.8 fusion.39
  8.3 0.7 convert_element_type.62
  9.0 1.1 fusion.27
  10.1 1.0 fusion.29
  11.3 0.9 select_reduce_fusion
  12.3 0.8 multiply_add_fusion.1
  13.2 0.5 convolution_convert_fusion.3
  14.0 75.3 %all_to_all.34 = bf16[32,2,7168]{2,1,0:T(2,128)(2,1)} all-to-all(bf16[32,2,7168]{2,1,0:T(2,128)(2,1)S(1)} %reshape.60), channel_id=1, replica_groups=mesh['groups'=2,'ep'=16,'tp'=4,'dp'=2] {'ep','dp'}, dimensions={0} | all-to-all | bytes 1835008 | tf_op jit(solution)/shard_map/all_to_all | solution.py:62
  89.5 0.5 convolution_convert_fusion.2
  90.3 54.1 %all_to_all.35 = bf16[32,2,7168]{2,1,0:T(2,128)(2,1)} all-to-all(bf16[32,2,7168]{2,1,0:T(2,128)(2,1)S(1)} %reshape.63), channel_id=1, replica_groups=mesh['groups'=2,'ep'=16,'tp'=4,'dp'=2] {'ep','dp'}, dimensions={0} | all-to-all | bytes 1835008 | tf_op jit(solution)/shard_map/all_to_all | solution.py:62
  144.5 8.4 %reshape.62 = bf16[256,7168]{1,0:T(8,128)(2,1)} reshape(bf16[16,4,2,2,7168]{4,3,2,1,0:T(2,128)(2,1)} %all-gather.3.cloned.1.call-done) | data formatting | bytes 7340032 | tf_op jit(solution)/shard_map/reshape | solution.py:75
  152.9 4.8 %fusion.10 = f32[256,256]{1,0:T(8,128)S(1)} fusion(bf16[256,7168]{1,0:T(8,128)(2,1)} %reshape.62, bf16[1,7168,256]{2,1,0:T(8,128)(2,1)} %param.11), kind=kOutput, calls=%fused_computation.16 | convolution fusion | flops 939524096 | bytes 7602176 | tf_op jit(solution)/shard_map/dot_general | solution.py:76
  157.8 0.9 copy-done.4
  158.7 1.1 fusion.21
  159.9 5.1 %convolution_convert_fusion.1 = bf16[16,4,2,2,7168]{4,0,3,2,1:T(8,128)(2,1)} fusion(bf16[1,256,7168]{2,1,0:T(8,128)(2,1)} %param.13, bf16[16,4,2,2,256]{4,3,2,1,0:T(2,128)(2,1)S(1)} %dot_general.41), kind=kOutput, calls=%fused_computation.1 | convolution fusion | flops 941359104 | bytes 7471104 | tf_op jit(solution)/shard_map/dot_general | solution.py:79
  165.2 21.5 %all-gather.5.cloned.1.call-done = bf16[16,4,2,2,7168]{4,3,2,1,0:T(2,128)(2,1)} async-done(((bf16[16,1,2,2,7168]{4,3,2,1,0:T(2,128)(2,1)}), bf16[16,4,2,2,7168]{4,3,2,1,0:T(2,128)(2,1)}) %all-gather.5.cloned.1.call-update) | async-done | bytes 3670032 | tf_op jit(solution)/shard_map/all_gather | solution.py:69
  186.7 8.4 %reshape.65 = bf16[256,7168]{1,0:T(8,128)(2,1)} reshape(bf16[16,4,2,2,7168]{4,3,2,1,0:T(2,128)(2,1)} %all-gather.5.cloned.1.call-done) | data formatting | bytes 7340032 | tf_op jit(solution)/shard_map/reshape | solution.py:75
  195.1 4.4 %fusion.8 = f32[256,256]{1,0:T(8,128)S(1)} fusion(bf16[256,7168]{1,0:T(8,128)(2,1)} %reshape.65, bf16[1,7168,256]{2,1,0:T(8,128)(2,1)} %param.11), kind=kOutput, calls=%fused_computation.14 | convolution fusion | flops 939524096 | bytes 7602176 | tf_op jit(solution)/shard_map/dot_general | solution.py:76
  199.5 0.9 copy-done.5
  200.4 1.1 fusion.18
  201.6 5.0 %convolution_convert_fusion = bf16[16,4,2,2,7168]{4,0,3,2,1:T(8,128)(2,1)} fusion(bf16[1,256,7168]{2,1,0:T(8,128)(2,1)} %param.13, bf16[16,4,2,2,256]{4,3,2,1,0:T(2,128)(2,1)S(1)} %dot_general.47), kind=kOutput, calls=%fused_computation | convolution fusion | flops 941359104 | bytes 7471104 | tf_op jit(solution)/shard_map/dot_general | solution.py:79
  206.6 31.7 %reduce-scatter.3.cloned.1.call-done = bf16[16,1,2,2,7168]{4,0,3,2,1:T(8,128)(2,1)} async-done(((bf16[16,4,2,2,7168]{4,0,3,2,1:T(8,128)(2,1)}), bf16[16,1,2,2,7168]{4,0,3,2,1:T(8,128)(2,1)}) %reduce-scatter.3.cloned.1.call-update) | async-done | bytes 917520 | tf_op jit(solution)/shard_map/reduce_scatter | solution.py:81
  238.4 3.1 copy.15
  241.5 13.3 %all-to-all-start.1 = ((bf16[32,2,7168]{2,1,0:T(2,128)(2,1)}), bf16[32,2,7168]{2,1,0:T(2,128)(2,1)S(1)}, u32[]{:S(2)}, u32[]{:S(2)}) async-start(bf16[32,2,7168]{2,1,0:T(2,128)(2,1)} %bitcast.6), calls=%async_computation.2 | async-start | bytes 1835008 | tf_op jit(solution)/shard_map/all_to_all | solution.py:85
  254.8 34.4 %reduce-scatter.5.cloned.1.call-done = bf16[16,1,2,2,7168]{4,0,3,2,1:T(8,128)(2,1)} async-done(((bf16[16,4,2,2,7168]{4,0,3,2,1:T(8,128)(2,1)}), bf16[16,1,2,2,7168]{4,0,3,2,1:T(8,128)(2,1)}) %reduce-scatter.5.cloned.1.call-update) | async-done | bytes 917520 | tf_op jit(solution)/shard_map/reduce_scatter | solution.py:81
  289.2 3.0 copy.17
  292.3 12.4 %all-to-all-done.1 = bf16[32,2,7168]{2,1,0:T(2,128)(2,1)S(1)} async-done(((bf16[32,2,7168]{2,1,0:T(2,128)(2,1)}), bf16[32,2,7168]{2,1,0:T(2,128)(2,1)S(1)}, u32[]{:S(2)}, u32[]{:S(2)}) %all-to-all-start.1) | async-done | bytes 917536 | tf_op jit(solution)/shard_map/all_to_all | solution.py:85
  304.7 4.3 %all-to-all-start.3 = ((bf16[32,2,7168]{2,1,0:T(2,128)(2,1)}), bf16[32,2,7168]{2,1,0:T(2,128)(2,1)S(1)}, u32[]{:S(2)}, u32[]{:S(2)}) async-start(bf16[32,2,7168]{2,1,0:T(2,128)(2,1)} %bitcast.10), calls=%async_computation.5 | async-start | bytes 1835008 | tf_op jit(solution)/shard_map/all_to_all | solution.py:85
  309.4 0.5 fusion
  309.9 49.2 %all-to-all-done.3 = bf16[32,2,7168]{2,1,0:T(2,128)(2,1)S(1)} async-done(((bf16[32,2,7168]{2,1,0:T(2,128)(2,1)}), bf16[32,2,7168]{2,1,0:T(2,128)(2,1)S(1)}, u32[]{:S(2)}, u32[]{:S(2)}) %all-to-all-start.3) | async-done | bytes 917536 | tf_op jit(solution)/shard_map/all_to_all | solution.py:85
  359.4 0.5 fusion.1
  359.9 0.7 pad_maximum_fusion
  (40 shorter events, 3.5 us)
Async XLA Ops:
  6.5 4.6 %copy-start = (bf16[7168,32]{0,1:T(8,128)(2,1)S(1)}, bf16[7168,32]{0,1:T(8,128)(2,1)}, u32[]{:S(2)}) copy-start(bf16[7168,32]{0,1:T(8,128)(2,1)} %param.9) | copy-start | bytes 1376260
  6.6 138.0 %all-gather.3.cloned.1.call-start = ((), (), s32[]{:S(2)}) async-start(), calls=%async_computation.6 | async-start | bytes 4587520 | tf_op jit(solution)/shard_map/all_gather | solution.py:69
  89.4 97.3 %all-gather.5.cloned.1.call-start = ((), (), s32[]{:S(2)}) async-start(), calls=%async_computation.8 | async-start | bytes 4587520 | tf_op jit(solution)/shard_map/all_gather | solution.py:69
  144.4 93.9 %reduce-scatter.3.cloned.1.call-start = ((), (), s32[]{:S(2)}) async-start(), calls=%async_computation.7 | async-start | bytes 4587520 | tf_op jit(solution)/shard_map/reduce_scatter | solution.py:81
  152.9 4.8 %copy-start.1 = (bf16[256,7168]{1,0:T(8,128)(2,1)S(1)}, bf16[256,7168]{1,0:T(8,128)(2,1)}, u32[]{:S(2)}) copy-start(bf16[256,7168]{1,0:T(8,128)(2,1)} %reshape.62) | copy-start | bytes 11010052
  152.9 5.7 %copy-start.4 = (bf16[1,7168,256]{2,1,0:T(8,128)(2,1)S(1)}, bf16[1,7168,256]{2,1,0:T(8,128)(2,1)}, u32[]{:S(2)}) copy-start(bf16[1,7168,256]{2,1,0:T(8,128)(2,1)} %param.12) | copy-start | bytes 11010052
  165.0 124.2 %reduce-scatter.5.cloned.1.call-start = ((), (), s32[]{:S(2)}) async-start(), calls=%async_computation.9 | async-start | bytes 4587520 | tf_op jit(solution)/shard_map/reduce_scatter | solution.py:81
  195.1 4.4 %copy-start.2 = (bf16[256,7168]{1,0:T(8,128)(2,1)S(1)}, bf16[256,7168]{1,0:T(8,128)(2,1)}, u32[]{:S(2)}) copy-start(bf16[256,7168]{1,0:T(8,128)(2,1)} %reshape.65) | copy-start | bytes 11010052
  195.1 5.3 %copy-start.5 = (bf16[1,7168,256]{2,1,0:T(8,128)(2,1)S(1)}, bf16[1,7168,256]{2,1,0:T(8,128)(2,1)}, u32[]{:S(2)}) copy-start(bf16[1,7168,256]{2,1,0:T(8,128)(2,1)} %param.12) | copy-start | bytes 11010052
  241.5 67.9 %copy-start.3 = (bf16[8,7168]{1,0:T(8,128)(2,1)S(1)}, bf16[8,7168]{1,0:T(8,128)(2,1)}, u32[]{:S(2)}) copy-start(bf16[8,7168]{1,0:T(8,128)(2,1)} %param.7) | copy-start | bytes 344068
  241.5 63.2 %all-to-all-start.1 = ((bf16[32,2,7168]{2,1,0:T(2,128)(2,1)}), bf16[32,2,7168]{2,1,0:T(2,128)(2,1)S(1)}, u32[]{:S(2)}, u32[]{:S(2)}) async-start(bf16[32,2,7168]{2,1,0:T(2,128)(2,1)} %bitcast.6), calls=%async_computation.2 | async-start | bytes 1835008 | tf_op jit(solution)/shard_map/all_to_all | solution.py:85
  304.7 54.4 %all-to-all-start.3 = ((bf16[32,2,7168]{2,1,0:T(2,128)(2,1)}), bf16[32,2,7168]{2,1,0:T(2,128)(2,1)S(1)}, u32[]{:S(2)}, u32[]{:S(2)}) async-start(bf16[32,2,7168]{2,1,0:T(2,128)(2,1)} %bitcast.10), calls=%async_computation.5 | async-start | bytes 1835008 | tf_op jit(solution)/shard_map/all_to_all | solution.py:85
Sparse Core Ops, SparseCore 0:
  89.5 42.1 all-gather.2
  144.6 42.1 all-gather.4
  189.3 49.0 reduce-scatter.2
  240.8 48.3 reduce-scatter.4
where the time goes:
time: 368 us; the launch traced here: 367 us
  waiting for transfers between devices  150 us (41%)
  blocking collectives  129 us (35%)
  local copies, waits for them, and re-layouts  27.4 us (7%)
  matrix products  23.5 us (6%)
  starting transfers between devices  18 us (5%)
  between operations  13.3 us (4%)
  other arithmetic  6.02 us (2%)
    all_to_all x2, blocking collectives, body(): lax.all_to_all(outgoing.reshape(ep_count * dp_count, capacity, feature_co...  129 us
    reduce_scatter x2, waiting for transfers between devices, body(): lax.psum_scatter(partial_value.astype(jnp.bfloat16), 'tp', scatter_dimens...  66.2 us
    all_to_all x2, waiting for transfers between devices, body(): lax.all_to_all(summed_local, ('ep', 'dp'), split_axis=0, concat_axis=0, t...  61.6 us
    all_gather x2, waiting for transfers between devices, body(): lax.all_gather(arrived.reshape(ep_count, 1, dp_count, capacity, feature_c...  21.5 us
    all_to_all x2, starting transfers between devices, body(): lax.all_to_all(summed_local, ('ep', 'dp'), split_axis=0, concat_axis=0, t...  17.6 us
    reshape x2, local copies, waits for them, and re-layouts, body(): row_block = portion.reshape(-1, feature_count)  16.8 us
    dot_general x2, matrix products, body(): jnp.dot(active, down_proj[0], preferred_element_type=jnp.float32)  10 us
    dot_general x2, matrix products, body(): jnp.dot(row_block, gate_proj[0], preferred_element_type=jnp.float32)  9.2 us
  transfers between devices with their start and end apart: 6, of which 5 were waited for; matrix products, arithmetic and copies ran while one was open for 12% of the time, Pallas kernels for 0%

commit v1 on v0

v1 whole, which is shorter than its diff:
```python
import jax
import jax.numpy as jnp
from jax import lax
from jax.sharding import PartitionSpec as P

GROUP = ("ep", "tp", "dp")
LANES = 128

route_scale = 2.827
norm_eps = 1e-06


def normalize(hidden, norm_gain):
    values = hidden.astype(jnp.float32)
    spread = jnp.mean(values * values, axis=-1, keepdims=True)
    return (values * lax.rsqrt(spread + norm_eps) * norm_gain.astype(jnp.float32)).astype(
        jnp.bfloat16
    )


def dense_weights(normed, router, expert_ids):
    logits = jnp.dot(normed, router, preferred_element_type=jnp.float32)
    scores = jax.nn.sigmoid(logits)
    expert_range = jnp.arange(router.shape[1], dtype=jnp.int32)
    chosen = jnp.any(expert_ids[:, :, None] == expert_range[None, None, :], axis=1)
    chosen_scores = jnp.where(chosen, scores, 0.0)
    return route_scale * chosen_scores / jnp.sum(chosen_scores, axis=-1, keepdims=True)


def weight_columns(weights):
    high = lax.reduce_precision(weights, exponent_bits=8, mantissa_bits=7)
    low = weights - high
    columns = jnp.concatenate([high, low], axis=1).astype(jnp.bfloat16)
    return jnp.pad(columns, ((0, 0), (0, LANES - columns.shape[1])))


def body(hidden, norm_gain, router, expert_ids, gate_proj, up_proj, down_proj):
    features = hidden.shape[1]
    experts = router.shape[1]
    normed = normalize(hidden, norm_gain)
    weights = dense_weights(normed, router, expert_ids)
    outgoing = jnp.concatenate([normed, weight_columns(weights)], axis=1)
    everyone = lax.all_gather(outgoing, GROUP, axis=0, tiled=True)
    rows = everyone[:, :features]
    own = lax.axis_index("ep") * lax.axis_size("dp") + lax.axis_index("dp")
    lane = jnp.arange(LANES, dtype=jnp.int32)
    own_lanes = (lane == own) | (lane == own + experts)
    columns = everyone[:, features:].astype(jnp.float32)
    weight = jnp.sum(jnp.where(own_lanes, columns, 0.0), axis=1, keepdims=True)
    gate_sum = jnp.dot(rows, gate_proj[0], preferred_element_type=jnp.float32)
    up_sum = jnp.dot(rows, up_proj[0], preferred_element_type=jnp.float32)
    active = (weight * (jax.nn.silu(gate_sum) * up_sum)).astype(jnp.bfloat16)
    partial_rows = jnp.dot(active, down_proj[0], preferred_element_type=jnp.float32)
    expert_sum = lax.psum_scatter(
        partial_rows.astype(jnp.bfloat16), GROUP, scatter_dimension=0, tiled=True
    )
    return (hidden.astype(jnp.float32) + expert_sum.astype(jnp.float32)).astype(jnp.bfloat16)


def solution(mesh):
    return jax.shard_map(
        body,
        mesh=mesh,
        in_specs=(
            P(("groups", "ep", "tp", "dp"), None),
            P(),
            P(),
            P(("groups", "ep", "tp", "dp"), None),
            P(("ep", "dp"), None, "tp"),
            P(("ep", "dp"), None, "tp"),
            P(("ep", "dp"), "tp", None),
        ),
        out_specs=P(("groups", "ep", "tp", "dp"), None),
        check_vma=False,
    )
```

time: 368 us -> 487 us (1.32); the launches traced: 367 us -> 477 us
  waiting for transfers between devices: 150 us -> 431 us
  blocking collectives: 129 us -> 0 us
  local copies, waits for them, and re-layouts: 27.4 us -> 0.02 us
  starting transfers between devices: 18 us -> 0.07 us
    reduce_scatter x2 -> x1, waiting for transfers between devices: 66.2 us -> 265 us  [body(): lax.psum_scatter(partial_rows.astype(jnp.bfloat16), GROUP, scatter_dimens...]
    all_gather x2 -> x1, waiting for transfers between devices: 21.5 us -> 166 us  [body(): everyone = lax.all_gather(outgoing, GROUP, axis=0, tiled=True)]
    all_to_all x2 -> x0, blocking collectives: 129 us -> none  [body(): lax.all_to_all(outgoing.reshape(ep_count * dp_count, capacity, feature_co...]
    all_to_all x2 -> x0, waiting for transfers between devices: 61.6 us -> none  [body(): lax.all_to_all(summed_local, ('ep', 'dp'), split_axis=0, concat_axis=0, t...]
    all_to_all x2 -> x0, starting transfers between devices: 17.6 us -> none  [body(): lax.all_to_all(summed_local, ('ep', 'dp'), split_axis=0, concat_axis=0, t...]
    reshape x4 -> x0, local copies, waits for them, and re-layouts: 17.5 us -> none  [the longest x2 16.8 us: body(): row_block = portion.reshape(-1, feature_count)]
    reduce_scatter x2 -> x0, local copies, waits for them, and re-layouts: 6.16 us -> none  [body(): lax.psum_scatter(partial_value.astype(jnp.bfloat16), 'tp', scatter_dimens...]
    dot_general x9 -> x3, matrix products: 13.5 us -> 18.2 us  [the longest x1 9.37 us: body(): up_sum = jnp.dot(rows, up_proj[0], preferred_element_type=jnp.float32)]
  transfers between devices with their start and end apart: 6 -> 2, of which waited for: 5 -> 2; matrix products, arithmetic and copies ran while one was open for 12% -> 0% of each run, Pallas kernels for 0% -> 0%
where the time goes in v1:
time: 487 us; the launch traced here: 477 us
  waiting for transfers between devices  431 us (89%)
  matrix products  25.6 us (5%)
  between operations  13.5 us (3%)
  other arithmetic  7.12 us (1%)
    reduce_scatter x1, waiting for transfers between devices, body(): lax.psum_scatter(partial_rows.astype(jnp.bfloat16), GROUP, scatter_dimens...  265 us
    all_gather x1, waiting for transfers between devices, body(): everyone = lax.all_gather(outgoing, GROUP, axis=0, tiled=True)  166 us
  transfers between devices with their start and end apart: 2, of which 2 were waited for; matrix products, arithmetic and copies ran while one was open for 0% of the time, Pallas kernels for 0%

profile of v1, /device:TPU:33, one launch (start us, length us, event | category | flops | bytes accessed | tf_op | source)
XLA Modules:
  0.0 477.5 jit_solution(16310504673255224288)
XLA Ops:
  6.5 0.0 copy-start
  6.6 0.0 all-gather.2.cloned.1.call-start
  6.6 1.1 fusion.26
  7.7 0.8 fusion.30
  8.5 0.7 convert_element_type.29
  9.2 1.0 fusion.28
  10.2 0.0 copy-done
  10.2 0.4 fusion.35
  10.6 0.1 reduce-precision_convert_fusion
  10.6 0.1 fusion.34
  10.7 0.7 pad_maximum_fusion
  11.4 0.1 all-gather.2.cloned.1.call-update
  11.4 0.1 reduce-scatter.2.cloned.1.call-start
  11.5 166.0 %all-gather.2.cloned.1.call-done = bf16[1024,7296]{1,0:T(8,128)(2,1)} async-done(((bf16[8,7296]{1,0:T(8,128)(2,1)}), bf16[1024,7296]{1,0:T(8,128)(2,1)}) %all-gather.2.cloned.1.call-update) | async-done | bytes 14942224 | tf_op jit(solution)/shard_map/all_gather | solution.py:43
  177.5 1.1 select_reduce_fusion
  178.6 0.0 copy-start.3
  178.6 8.5 %fusion.2 = f32[1024,256]{1,0:T(8,128)S(1)} fusion(bf16[1024,7296]{1,0:T(8,128)(2,1)} %all-gather.2.cloned.1.call-done, bf16[1,7168,256]{2,1,0:T(8,128)(2,1)} %param.11), kind=kOutput, calls=%fused_computation.3 | convolution fusion | flops 3758096384 | bytes 19398656 | tf_op jit(solution)/shard_map/dot_general | solution.py:50
  187.1 0.0 copy-done.3
  187.1 0.0 copy-start.1
  187.1 9.4 %fusion.17 = bf16[1024,256]{1,0:T(8,128)(2,1)S(1)} fusion(bf16[1,7168,256]{2,1,0:T(8,128)(2,1)S(1)} %copy-done.3, bf16[1024,7296]{1,0:T(8,128)(2,1)} %all-gather.2.cloned.1.call-done, f32[1024,256]{1,0:T(8,128)S(1)} %fusion.2, f32[1024]{0:T(1024)S(1)} %select_reduce_fusion), kind=kOutput, calls=%fused_computation.10 | convolution fusion | flops 3759931392 | bytes 19927040 | tf_op jit(solution)/shard_map/dot_general | solution.py:51
  196.5 0.0 copy-done.1
  196.5 0.0 copy-start.2
  196.5 7.4 %convolution_convert_fusion = bf16[1024,7168]{1,0:T(8,128)(2,1)} fusion(bf16[1024,256]{1,0:T(8,128)(2,1)S(1)} %fusion.17, bf16[1,256,7168]{2,1,0:T(8,128)(2,1)S(1)} %copy-done.1), kind=kOutput, calls=%fused_computation | convolution fusion | flops 3765436416 | bytes 18874368 | tf_op jit(solution)/shard_map/dot_general | solution.py:53
  203.9 0.1 reduce-scatter.2.cloned.1.call-update
  203.9 265.1 %reduce-scatter.2.cloned.1.call-done = bf16[8,7168]{1,0:T(8,128)(2,1)} async-done(((bf16[1024,7168]{1,0:T(8,128)(2,1)}), bf16[8,7168]{1,0:T(8,128)(2,1)}) %reduce-scatter.2.cloned.1.call-update) | async-done | bytes 114704 | tf_op jit(solution)/shard_map/reduce_scatter | solution.py:54
  469.0 0.0 copy-done.2
  469.0 1.6 fusion.29
  (2 shorter events, 0.0 us)
Async XLA Ops:
  6.5 3.6 copy-start
  6.6 171.0 %all-gather.2.cloned.1.call-start = ((), (), s32[]{:S(2)}) async-start(), calls=%async_computation.1 | async-start | bytes 15058944 | tf_op jit(solution)/shard_map/all_gather | solution.py:43
  11.4 457.6 %reduce-scatter.2.cloned.1.call-start = ((), (), s32[]{:S(2)}) async-start(), calls=%async_computation.2 | async-start | bytes 14794752 | tf_op jit(solution)/shard_map/reduce_scatter | solution.py:54
  178.6 8.5 %copy-start.3 = (bf16[1,7168,256]{2,1,0:T(8,128)(2,1)S(1)}, bf16[1,7168,256]{2,1,0:T(8,128)(2,1)}, u32[]{:S(2)}) copy-start(bf16[1,7168,256]{2,1,0:T(8,128)(2,1)} %param.12) | copy-start | bytes 11010052
  187.1 9.4 %copy-start.1 = (bf16[1,256,7168]{2,1,0:T(8,128)(2,1)S(1)}, bf16[1,256,7168]{2,1,0:T(8,128)(2,1)}, u32[]{:S(2)}) copy-start(bf16[1,256,7168]{2,1,0:T(8,128)(2,1)} %param.13) | copy-start | bytes 11010052
  196.5 272.6 %copy-start.2 = (bf16[8,7168]{1,0:T(8,128)(2,1)S(1)}, bf16[8,7168]{1,0:T(8,128)(2,1)}, u32[]{:S(2)}) copy-start(bf16[8,7168]{1,0:T(8,128)(2,1)} %param.7) | copy-start | bytes 344068
Sparse Core Ops, SparseCore 0:
  11.6 165.9 all-gather.1
  204.1 264.9 reduce-scatter.1
